TPU v7x, 32 devices: a whole 2x2x4 slice. The times are simulated.
32 devices in a mesh: rep: 4 (over y, x), dom: 8 (over z, core).
Axes of the slice: x: 2, y: 2, z: 4, core: 2. Of those that a mesh axis runs over, the one named last changes fastest.
Arguments:
- node_pos: float32 [3, 16384], P(None, 'dom'), may hold values from -6 to 6
- node_order: int32 [8, 2048], P('dom'), may hold values from 0 to 2047, each once within a row
- facet_centroid: float32 [3, 16384], P(None, 'dom'), may hold values from -6 to 6
- facet_normal: float32 [3, 16384], P(None, 'dom'), may hold values from -6 to 6
- facet_nodes: int32 [3, 16384], P(None, 'dom'), may hold values from 0 to 2047
- pair_bucket: int32 [4, 8, 128], P('rep', 'dom'), may hold values from 0 to 15
- pair_owner: int32 [4, 8, 128, 1], P('rep', 'dom'), may hold values from 0 to 7; in each aligned block of 128 rows (0 to 127, 128 to 255, ..., all dimensions but the last counted through in order) at most 32 rows name the same one
- pair_slot: int32 [4, 8, 128], P('rep', 'dom'), may hold values from 0 to 15
- pair_count: int32 [4, 8], P('rep', 'dom'), may hold values from 64 to 128, as said below
Outputs:
- node_force: float32 [3, 16384], P(None, 'dom')
Inputs may be any that keep to these rules, and one draw needn't show every extreme that they name: `pair_owner`: among the 128 pairs of one device, each domain is named at most 32 times, and exactly 32 times in some device's pairs. `pair_count`: some device uses all 128 pairs. `node_order`: each row is a permutation.
All inputs are finite; a program needn't handle non-finite values.
Results may differ from a plain program's by a relative error of at most 0.00013.
Values sent between devices are 32-bit elements; how exact they have to be, the bound alone decides.
A program may use at most 64 MiB of HBM per device.

v0:
```python
import jax
import jax.numpy as jnp
from jax import lax
from jax.sharding import PartitionSpec as P

BUCKET = 128
PAIRS_DEV = 128
STIFFNESS = 0.125
RADIUS_SQ = 4.0
pair_block = 8


def tile_terms(facet_geom, node_points):
    centre = facet_geom[:, 0:3]
    normal = facet_geom[:, 3:6]
    delta = node_points[:, :, None, :] - centre[:, :, :, None]
    gap = jnp.sum(normal[:, :, :, None] * delta, axis=1)
    dist = jnp.sum(delta * delta, axis=1)
    strength = STIFFNESS * jax.nn.softplus(-gap) * jnp.exp(-dist / RADIUS_SQ)
    node_term = jnp.einsum("bkf,bfp->bkp", normal, strength, precision=lax.Precision.HIGHEST)
    reaction = -normal * jnp.sum(strength, axis=2)[:, None, :]
    return (node_term, reaction)


def slot_numbers(owners, is_live, per_owner, dummy_slot):
    rows = owners.shape[0]
    positions = jnp.arange(rows, dtype=jnp.int32)
    earlier = (
        (positions[None, :] < positions[:, None])
        & (owners[None, :] == owners[:, None])
        & is_live[None, :]
    )
    ranking = jnp.sum(earlier.astype(jnp.int32), axis=1)
    return jnp.where(is_live, owners * per_owner + ranking, dummy_slot)


def pair_loop(
    live_count, geom_rows, point_rows, slot_index, bucket_index, is_live, slot_total, bucket_total
):
    width = geom_rows.shape[2]
    geom_pad = jnp.concatenate([geom_rows, jnp.zeros((pair_block, 6, width), jnp.float32)], 0)
    point_pad = jnp.concatenate([point_rows, jnp.zeros((pair_block, 3, width), jnp.float32)], 0)
    slot_pad = jnp.concatenate([slot_index, jnp.full((pair_block,), slot_total, jnp.int32)])
    bucket_pad = jnp.concatenate([bucket_index, jnp.zeros((pair_block,), jnp.int32)])
    live_pad = jnp.concatenate([is_live, jnp.zeros((pair_block,), jnp.bool_)])

    def step(block_index, carry):
        slot_acc, bucket_acc = carry
        start = block_index * pair_block
        facet_geom = lax.dynamic_slice_in_dim(geom_pad, start, pair_block)
        node_points = lax.dynamic_slice_in_dim(point_pad, start, pair_block)
        slot_take = lax.dynamic_slice_in_dim(slot_pad, start, pair_block)
        bucket_take = lax.dynamic_slice_in_dim(bucket_pad, start, pair_block)
        weight = lax.dynamic_slice_in_dim(live_pad, start, pair_block).astype(jnp.float32)
        node_term, reaction = tile_terms(facet_geom, node_points)
        slot_acc = slot_acc.at[slot_take].add(node_term * weight[:, None, None])
        bucket_acc = bucket_acc.at[bucket_take].add(reaction * weight[:, None, None])
        return (slot_acc, bucket_acc)

    blocks = (live_count + pair_block - 1) // pair_block
    start_acc = (
        jnp.zeros((slot_total + 1, 3, width), jnp.float32),
        jnp.zeros((bucket_total, 3, width), jnp.float32),
    )
    return lax.fori_loop(jnp.int32(0), blocks, step, start_acc)


def per_device(
    node_pos,
    node_order,
    facet_centroid,
    facet_normal,
    facet_nodes,
    pair_bucket,
    pair_owner,
    pair_slot,
    pair_count,
):
    domains = lax.axis_size("dom")
    per_owner = max(2, 2 * PAIRS_DEV // domains)
    slot_total = domains * per_owner
    width = BUCKET
    node_buckets = node_pos.shape[1] // width
    facet_buckets = facet_centroid.shape[1] // width
    bucket_points = node_pos[:, node_order[0]].reshape(3, node_buckets, width).transpose(1, 0, 2)
    bucket_geom = (
        jnp.concatenate([facet_centroid, facet_normal], 0)
        .reshape(6, facet_buckets, width)
        .transpose(1, 0, 2)
    )
    owners = pair_owner[0, 0, :, 0]
    buckets = pair_bucket[0, 0]
    slots = pair_slot[0, 0]
    rows = buckets.shape[0]
    positions = jnp.arange(rows, dtype=jnp.int32)
    is_live = positions < pair_count[0, 0]
    live_count = jnp.sum(is_live.astype(jnp.int32))
    slot_index = slot_numbers(owners, is_live, per_owner, slot_total)
    request = (
        jnp.full((slot_total + 1,), -1, jnp.int32)
        .at[slot_index]
        .set(slots)[:-1]
        .reshape(domains, per_owner)
    )
    every_bucket = lax.all_gather(bucket_points, "dom", axis=0, tiled=True)
    point_rows = every_bucket[owners * node_buckets + slots]
    slot_acc, facet_acc = pair_loop(
        live_count,
        bucket_geom[buckets],
        point_rows,
        slot_index,
        buckets,
        is_live,
        slot_total,
        facet_buckets,
    )
    home_blocks, home_slots = (
        lax.all_to_all(
            slot_acc[:-1].reshape(domains, per_owner, 3, width),
            "dom",
            split_axis=0,
            concat_axis=0,
            tiled=True,
        ),
        lax.all_to_all(request.astype(jnp.float32), "dom", split_axis=0, concat_axis=0, tiled=True),
    )
    home_slots = home_slots.reshape(slot_total).astype(jnp.int32)
    home_blocks = home_blocks.reshape(slot_total, 3, width)
    target = jnp.where(home_slots >= 0, home_slots, node_buckets)
    bucket_force = (
        jnp.zeros((node_buckets + 1, 3, width), jnp.float32).at[target].add(home_blocks)[:-1]
    )
    node_force = (
        jnp.zeros((3, node_pos.shape[1]), jnp.float32)
        .at[:, node_order[0]]
        .add(bucket_force.transpose(1, 0, 2).reshape(3, -1))
    )
    reaction = facet_acc.transpose(1, 0, 2).reshape(3, -1) / 3.0
    for corner in range(3):
        node_force = node_force.at[:, facet_nodes[corner]].add(reaction)
    return lax.psum(node_force, "rep")


def solution(mesh):
    placed = (
        P(None, "dom"),
        P("dom", None),
        P(None, "dom"),
        P(None, "dom"),
        P(None, "dom"),
        P("rep", "dom", None),
        P("rep", "dom", None, None),
        P("rep", "dom", None),
        P("rep", "dom"),
    )
    return jax.shard_map(
        per_device, mesh=mesh, in_specs=placed, out_specs=P(None, "dom"), check_vma=False
    )
```

profile of v0, /device:TPU:0, one launch (start us, length us, event | category | flops | bytes accessed | tf_op | source)
XLA Modules:
  0.0 215.3 jit_solution(11657129899521065713)
XLA Ops:
  2.3 1.1 scatter_custom_fusion.2
  4.1 6.4 %all-to-all-start = ((f32[8,1,32]{2,1,0:T(1,128)}), f32[8,1,32]{2,1,0:T(1,128)S(1)}, u32[]{:S(2)}, u32[]{:S(2)}) async-start(f32[8,1,32]{2,1,0:T(1,128)} %convert_element_type.37), calls=%async_computation | async-start | bytes 8192 | tf_op jit(solution)/shard_map/all_to_all | solution.py:125
  12.4 1.1 copy.46
  13.5 5.5 %gather_fusion.1 = f32[2048,3]{1,0:T(8,128)S(1)} fusion(f32[3,2048]{0,1:T(8,128)S(1)} %copy.46, s32[2048]{0:T(1024)S(1)} %broadcast_clamp_fusion), kind=kCustom, calls=%fused_computation.1 | custom fusion | bytes 57344 | tf_op jit(solution)/shard_map/gather | solution.py:85
  19.3 14.8 %all_gather.3 = f32[128,3,128]{2,0,1:T(8,128)S(1)} all-gather(f32[16,3,128]{2,0,1:T(8,128)S(1)} %bitcast.77), channel_id=1, replica_groups=mesh['rep'=4,'dom'=8] {'dom'}, dimensions={0}, use_global_device_ids=true | all-gather | bytes 221184 | tf_op jit(solution)/shard_map/all_gather | solution.py:105
  36.1 62.5 %while.12 = (s32[]{:T(128)}, f32[257,3,128]{2,1,0:T(4,128)S(1)}, f32[16,3,128]{2,1,0:T(4,128)S(1)}, s32[]{:T(128)}, s32[136]{0:T(256)S(1)}, /*index=5*/f32[136,6...) while((s32[]{:T(128)}, f32[257,3,128]{2,1,0:T(4,128)S(1)}, ...), condition=%wide.region_9.10_spmd, body=%wide.region_3.9_spmd.sunk | while | flops 8012863 | bytes 3387895 | solution.py:65
  36.1 1.0 fusion.23
  40.1 1.0 fusion.23
  44.0 1.0 fusion.23
  47.9 1.0 fusion.23
  63.5 1.0 fusion.23
  67.4 1.0 fusion.23
  71.3 1.0 fusion.23
  79.1 1.0 fusion.23
  90.8 1.0 fusion.23
  94.7 1.0 fusion.23
  99.8 3.5 %all-to-all-start.1 = ((f32[8,32,3,128]{3,1,2,0:T(8,128)}), f32[8,32,3,128]{3,1,2,0:T(8,128)S(1)}, u32[]{:S(2)}, u32[]{:S(2)}) async-start(f32[8,32,3,128]{3,1,2,0:T(8,128)} %copy.50), calls=%async_computation.1 | async-start | bytes 786432 | tf_op jit(solution)/shard_map/all_to_all | solution.py:118
  103.5 12.3 %all-to-all-done.1 = f32[8,32,3,128]{3,1,2,0:T(8,128)S(1)} async-done(((f32[8,32,3,128]{3,1,2,0:T(8,128)}), f32[8,32,3,128]{3,1,2,0:T(8,128)S(1)}, u32[]{:S(2)}, u32[]{:S(2)}) %all-to-all-start.1) | async-done | bytes 393248 | tf_op jit(solution)/shard_map/all_to_all | solution.py:118
  116.1 8.9 %scatter_fusion.2 = f32[17,3,128]{2,1,0:T(4,128)S(1)} fusion(f32[17,3,128]{2,1,0:T(4,128)S(1)} %broadcast_in_dim.32, s32[256]{0:T(256)S(1)} %bitcast.84, f32[256,3,128]{2,1,0:T(4,128)S(1)} %copy.52), kind=kCustom, calls=%fused_computation.6 | custom fusion | flops 98304 | bytes 1180672 | tf_op jit(solution)/shard_map/scatter-add | solution.py:131
  125.3 11.7 %scatter_custom_fusion.4 = f32[3,2048]{0,1:T(8,128)S(1)} fusion(s32[2048]{0:T(1024)S(1)} %bitcast.82, f32[2048,3]{1,0:T(8,128)S(1)} %copy.53, f32[]{:T(128)} %constant.33.clone.1), kind=kCustom, calls=%fused_computation.26 | custom fusion | flops 6144 | bytes 24580 | tf_op jit(solution)/shard_map/scatter-add | solution.py:136
  137.1 11.9 %scatter_fusion.3 = f32[3,2048]{0,1:T(8,128)S(1)} fusion(f32[3,2048]{0,1:T(8,128)S(1)} %scatter_custom_fusion.4, s32[2048]{0:T(1024)S(1)} %bitcast.80, f32[2048,3]{1,0:T(8,128)S(1)} %copy.54), kind=kCustom, calls=%fused_computation.8 | custom fusion | flops 6144 | bytes 81920 | tf_op jit(solution)/shard_map/scatter-add | solution.py:140
  148.9 12.1 %scatter_fusion.4 = f32[3,2048]{0,1:T(8,128)S(1)} fusion(f32[3,2048]{0,1:T(8,128)S(1)} %scatter_fusion.3, s32[2048]{0:T(1024)S(1)} %bitcast.79, f32[2048,3]{1,0:T(8,128)S(1)} %copy.54), kind=kCustom, calls=%fused_computation.9 | custom fusion | flops 6144 | bytes 81920 | tf_op jit(solution)/shard_map/scatter-add | solution.py:140
  161.0 11.9 %scatter_fusion.5 = f32[3,2048]{0,1:T(8,128)S(1)} fusion(f32[3,2048]{0,1:T(8,128)S(1)} %scatter_fusion.4, s32[2048]{0:T(1024)S(1)} %bitcast.78, f32[2048,3]{1,0:T(8,128)S(1)} %copy.54), kind=kCustom, calls=%fused_computation.10 | custom fusion | flops 6144 | bytes 81920 | tf_op jit(solution)/shard_map/scatter-add | solution.py:140
  172.9 41.5 %psum.7 = f32[3,2048]{0,1:T(8,128)S(1)} all-reduce(f32[3,2048]{0,1:T(8,128)S(1)} %scatter_fusion.5), channel_id=1, replica_groups=mesh['rep'=4,'dom'=8] {'rep'}, use_global_device_ids=true, to_apply=%region_15.16 | all-reduce | flops 6144 | bytes 49152 | tf_op jit(solution)/shard_map/psum | solution.py:141
  (184 shorter events, 59.9 us)
Async XLA Ops:
  4.1 95.8 %all-to-all-start = ((f32[8,1,32]{2,1,0:T(1,128)}), f32[8,1,32]{2,1,0:T(1,128)S(1)}, u32[]{:S(2)}, u32[]{:S(2)}) async-start(f32[8,1,32]{2,1,0:T(1,128)} %convert_element_type.37), calls=%async_computation | async-start | bytes 8192 | tf_op jit(solution)/shard_map/all_to_all | solution.py:125
  13.5 20.7 %copy-start.3 = (s32[1,1,128,1]{2,3,1,0:T(1,128)S(1)}, s32[1,1,128,1]{2,3,1,0:T(1,128)}, u32[]{:S(2)}) copy-start(s32[1,1,128,1]{2,3,1,0:T(1,128)} %param.17) | copy-start | bytes 1540
  13.5 20.8 %copy-start.4 = (s32[1,1,128]{2,1,0:T(1,128)S(1)}, s32[1,1,128]{2,1,0:T(1,128)}, u32[]{:S(2)}) copy-start(s32[1,1,128]{2,1,0:T(1,128)} %param.16) | copy-start | bytes 1540
  19.3 15.8 %copy-start = (f32[3,2048]{1,0:T(4,128)S(1)}, f32[3,2048]{1,0:T(4,128)}, u32[]{:S(2)}) copy-start(f32[3,2048]{1,0:T(4,128)} %param.14) | copy-start | bytes 73732
  19.3 15.8 %copy-start.1 = (f32[3,2048]{1,0:T(4,128)S(1)}, f32[3,2048]{1,0:T(4,128)}, u32[]{:S(2)}) copy-start(f32[3,2048]{1,0:T(4,128)} %param.13) | copy-start | bytes 73732
  99.5 3.9 %copy-start.2 = (s32[3,2048]{1,0:T(4,128)S(1)}, s32[3,2048]{1,0:T(4,128)}, u32[]{:S(2)}) copy-start(s32[3,2048]{1,0:T(4,128)} %param.15) | copy-start | bytes 73732
  99.8 15.9 %all-to-all-start.1 = ((f32[8,32,3,128]{3,1,2,0:T(8,128)}), f32[8,32,3,128]{3,1,2,0:T(8,128)S(1)}, u32[]{:S(2)}, u32[]{:S(2)}) async-start(f32[8,32,3,128]{3,1,2,0:T(8,128)} %copy.50), calls=%async_computation.1 | async-start | bytes 786432 | tf_op jit(solution)/shard_map/all_to_all | solution.py:118
where the time goes:
time: 216 us; the launch traced here: 215 us
  other arithmetic  112 us (52%)
  blocking collectives  56.2 us (26%)
  local copies, waits for them, and re-layouts  13.8 us (6%)
  waiting for transfers between devices  12.3 us (6%)
  starting transfers between devices  9.82 us (5%)
  matrix products  8.35 us (4%)
    psum x1, blocking collectives, per_device(): return lax.psum(node_force, 'rep')  41.5 us
    scatter-add x3, other arithmetic, per_device(): node_force = node_force.at[:, facet_nodes[corner]].add(reaction)  35.8 us
    reduce_sum x16, other arithmetic, tile_terms(): gap = jnp.sum(normal[:, :, :, None] * delta, axis=1)  16.6 us
    all_gather x1, blocking collectives, per_device(): every_bucket = lax.all_gather(bucket_points, 'dom', axis=0, tiled=True)  14.8 us
    scatter-add x16, other arithmetic, step(): slot_acc = slot_acc.at[slot_take].add(node_term * weight[:, None, None])  12.5 us
    scatter-add x16, other arithmetic, step(): bucket_acc.at[bucket_take].add(reaction * weight[:, None, None])  12.5 us
    all_to_all x1, waiting for transfers between devices, per_device(): lax.all_to_all(slot_acc[:-1].reshape(domains, per_owner, 3, width), 'dom'...  12.3 us
    scatter-add x1, other arithmetic, per_device(): node_force = jnp.zeros((3, node_pos.shape[1]), jnp.float32).at[:, node_or...  11.7 us
  transfers between devices with their start and end apart: 2, of which 1 were waited for; matrix products, arithmetic and copies ran while one was open for 34% of the time, Pallas kernels for 0%

commit v1 on v0

--- a/solution.py
+++ b/solution.py
@@ -102,7 +102,12 @@
         .set(slots)[:-1]
         .reshape(domains, per_owner)
     )
-    every_bucket = lax.all_gather(bucket_points, "dom", axis=0, tiled=True)
+    ring = [bucket_points]
+    for hop in range(7):
+        ring.append(lax.ppermute(ring[-1], "dom", [(dev, (dev + 1) % 8) for dev in range(8)]))
+    every_bucket = jnp.roll(
+        jnp.concatenate(ring[::-1], axis=0), (lax.axis_index("dom") + 1) * ring[0].shape[0], axis=0
+    )
     point_rows = every_bucket[owners * node_buckets + slots]
     slot_acc, facet_acc = pair_loop(
         live_count,

time: 216 us -> 226 us (1.046)
  waiting for transfers between devices: 12.3 us -> 38.9 us
  blocking collectives: 56.2 us -> 41.3 us
    ppermute x0 -> x7, waiting for transfers between devices: none -> 26.9 us  [per_device(): lax.ppermute(ring[-1], 'dom', [(dev, (dev + 1) % 8) for dev in range(8)])]
    all_gather x1 -> x0, blocking collectives: 14.8 us -> none  [per_device(): every_bucket = lax.all_gather(bucket_points, 'dom', axis=0, tiled=True)]
  transfers between devices with their start and end apart: 2 -> 9, of which waited for: 1 -> 7; matrix products, arithmetic and copies ran while one was open for 34% -> 30% of each run, Pallas kernels for 0% -> 0%
where the time goes in v1:
time: 226 us; the launch traced here: 225 us
  other arithmetic  111 us (49%)
  blocking collectives  41.3 us (18%)
  waiting for transfers between devices  38.9 us (17%)
  local copies, waits for them, and re-layouts  13.8 us (6%)
  starting transfers between devices  9.3 us (4%)
  matrix products  8.35 us (4%)
    psum x1, blocking collectives, per_device(): return lax.psum(node_force, 'rep')  41.3 us
    scatter-add x3, other arithmetic, per_device(): node_force = node_force.at[:, facet_nodes[corner]].add(reaction)  35.8 us
    ppermute x7, waiting for transfers between devices, per_device(): lax.ppermute(ring[-1], 'dom', [(dev, (dev + 1) % 8) for dev in range(8)])  26.9 us
    reduce_sum x16, other arithmetic, tile_terms(): gap = jnp.sum(normal[:, :, :, None] * delta, axis=1)  16.6 us
    scatter-add x16, other arithmetic, step(): slot_acc = slot_acc.at[slot_take].add(node_term * weight[:, None, None])  12.5 us
    scatter-add x16, other arithmetic, step(): bucket_acc.at[bucket_take].add(reaction * weight[:, None, None])  12.5 us
    all_to_all x1, waiting for transfers between devices, per_device(): lax.all_to_all(slot_acc[:-1].reshape(domains, per_owner, 3, width), 'dom'...  12 us
    scatter-add x1, other arithmetic, per_device(): node_force = jnp.zeros((3, node_pos.shape[1]), jnp.float32).at[:, node_or...  11.7 us
  transfers between devices with their start and end apart: 9, of which 7 were waited for; matrix products, arithmetic and copies ran while one was open for 30% of the time, Pallas kernels for 0%

profile of v1, /device:TPU:0, one launch (start us, length us, event | category | flops | bytes accessed | tf_op | source)
XLA Modules:
  0.0 225.1 jit_solution(9492872087476215533)
XLA Ops:
  0.8 1.1 copy.44
  1.9 5.5 %gather_fusion.1 = f32[2048,3]{1,0:T(8,128)S(1)} fusion(f32[3,2048]{0,1:T(8,128)S(1)} %copy.44, s32[2048]{0:T(1024)S(1)} %broadcast_clamp_fusion), kind=kCustom, calls=%fused_computation.1 | custom fusion | bytes 57344 | tf_op jit(solution)/shard_map/gather | solution.py:85
  10.1 3.8 %collective-permute-done = f32[16,3,128]{2,1,0:T(4,128)S(1)} collective-permute-done((f32[16,3,128]{2,1,0:T(4,128)S(1)}, f32[16,3,128]{2,1,0:T(4,128)S(1)}, u32[]{:S(2)}, u32[]{:S(2)}) %collective-permute-start) | collective-permute-done | bytes 24608 | tf_op jit(solution)/shard_map/ppermute | solution.py:107
  14.6 4.8 %all-to-all-start = ((f32[8,1,32]{2,1,0:T(1,128)}), f32[8,1,32]{2,1,0:T(1,128)S(1)}, u32[]{:S(2)}, u32[]{:S(2)}) async-start(f32[8,1,32]{2,1,0:T(1,128)} %convert_element_type.37), calls=%async_computation | async-start | bytes 8192 | tf_op jit(solution)/shard_map/all_to_all | solution.py:130
  19.9 4.8 %collective-permute-done.2 = f32[16,3,128]{2,1,0:T(4,128)S(1)} collective-permute-done((f32[16,3,128]{2,1,0:T(4,128)S(1)}, f32[16,3,128]{2,1,0:T(4,128)S(1)}, u32[]{:S(2)}, u32[]{:S(2)}) %collective-permute-start.2) | collective-permute-done | bytes 24608 | tf_op jit(solution)/shard_map/ppermute | solution.py:107
  25.3 4.5 %collective-permute-done.3 = f32[16,3,128]{2,1,0:T(4,128)S(1)} collective-permute-done((f32[16,3,128]{2,1,0:T(4,128)S(1)}, f32[16,3,128]{2,1,0:T(4,128)S(1)}, u32[]{:S(2)}, u32[]{:S(2)}) %collective-permute-start.3) | collective-permute-done | bytes 24608 | tf_op jit(solution)/shard_map/ppermute | solution.py:107
  29.8 5.1 %collective-permute-done.4 = f32[16,3,128]{2,1,0:T(4,128)S(1)} collective-permute-done((f32[16,3,128]{2,1,0:T(4,128)S(1)}, f32[16,3,128]{2,1,0:T(4,128)S(1)}, u32[]{:S(2)}, u32[]{:S(2)}) %collective-permute-start.4) | collective-permute-done | bytes 24608 | tf_op jit(solution)/shard_map/ppermute | solution.py:107
  35.0 5.1 %collective-permute-done.5 = f32[16,3,128]{2,1,0:T(4,128)S(1)} collective-permute-done((f32[16,3,128]{2,1,0:T(4,128)S(1)}, f32[16,3,128]{2,1,0:T(4,128)S(1)}, u32[]{:S(2)}, u32[]{:S(2)}) %collective-permute-start.5) | collective-permute-done | bytes 24608 | tf_op jit(solution)/shard_map/ppermute | solution.py:107
  41.6 3.7 %collective-permute-done.6 = f32[16,3,128]{2,1,0:T(4,128)S(1)} collective-permute-done((f32[16,3,128]{2,1,0:T(4,128)S(1)}, f32[16,3,128]{2,1,0:T(4,128)S(1)}, u32[]{:S(2)}, u32[]{:S(2)}) %collective-permute-start.6) | collective-permute-done | bytes 24608 | tf_op jit(solution)/shard_map/ppermute | solution.py:107
  46.5 62.5 %while.12 = (s32[]{:T(128)}, f32[257,3,128]{2,1,0:T(4,128)S(1)}, f32[16,3,128]{2,1,0:T(4,128)S(1)}, s32[]{:T(128)}, s32[136]{0:T(256)S(1)}, /*index=5*/f32[136,6...) while((s32[]{:T(128)}, f32[257,3,128]{2,1,0:T(4,128)S(1)}, ...), condition=%wide.region_9.10_spmd, body=%wide.region_3.9_spmd.sunk | while | flops 8012863 | bytes 3387895 | solution.py:65
  46.6 1.0 fusion.23
  62.2 1.0 fusion.23
  70.0 1.0 fusion.23
  77.8 1.0 fusion.23
  81.7 1.0 fusion.23
  85.6 1.0 fusion.23
  109.8 3.5 %all-to-all-start.1 = ((f32[8,32,3,128]{3,1,2,0:T(8,128)}), f32[8,32,3,128]{3,1,2,0:T(8,128)S(1)}, u32[]{:S(2)}, u32[]{:S(2)}) async-start(f32[8,32,3,128]{3,1,2,0:T(8,128)} %copy.47), calls=%async_computation.1 | async-start | bytes 786432 | tf_op jit(solution)/shard_map/all_to_all | solution.py:123
  113.8 12.0 %all-to-all-done.1 = f32[8,32,3,128]{3,1,2,0:T(8,128)S(1)} async-done(((f32[8,32,3,128]{3,1,2,0:T(8,128)}), f32[8,32,3,128]{3,1,2,0:T(8,128)S(1)}, u32[]{:S(2)}, u32[]{:S(2)}) %all-to-all-start.1) | async-done | bytes 393248 | tf_op jit(solution)/shard_map/all_to_all | solution.py:123
  126.1 8.9 %scatter_fusion.2 = f32[17,3,128]{2,1,0:T(4,128)S(1)} fusion(f32[17,3,128]{2,1,0:T(4,128)S(1)} %broadcast_in_dim.32, s32[256]{0:T(256)S(1)} %bitcast.85, f32[256,3,128]{2,1,0:T(4,128)S(1)} %copy.49), kind=kCustom, calls=%fused_computation.6 | custom fusion | flops 98304 | bytes 1180672 | tf_op jit(solution)/shard_map/scatter-add | solution.py:136
  135.3 11.7 %scatter_custom_fusion.4 = f32[3,2048]{0,1:T(8,128)S(1)} fusion(s32[2048]{0:T(1024)S(1)} %bitcast.83, f32[2048,3]{1,0:T(8,128)S(1)} %copy.50, f32[]{:T(128)} %constant.43.clone.1), kind=kCustom, calls=%fused_computation.26 | custom fusion | flops 6144 | bytes 24580 | tf_op jit(solution)/shard_map/scatter-add | solution.py:141
  147.0 11.9 %scatter_fusion.3 = f32[3,2048]{0,1:T(8,128)S(1)} fusion(f32[3,2048]{0,1:T(8,128)S(1)} %scatter_custom_fusion.4, s32[2048]{0:T(1024)S(1)} %bitcast.81, f32[2048,3]{1,0:T(8,128)S(1)} %copy.51), kind=kCustom, calls=%fused_computation.8 | custom fusion | flops 6144 | bytes 81920 | tf_op jit(solution)/shard_map/scatter-add | solution.py:145
  158.9 12.1 %scatter_fusion.4 = f32[3,2048]{0,1:T(8,128)S(1)} fusion(f32[3,2048]{0,1:T(8,128)S(1)} %scatter_fusion.3, s32[2048]{0:T(1024)S(1)} %bitcast.80, f32[2048,3]{1,0:T(8,128)S(1)} %copy.51), kind=kCustom, calls=%fused_computation.9 | custom fusion | flops 6144 | bytes 81920 | tf_op jit(solution)/shard_map/scatter-add | solution.py:145
  171.0 11.9 %scatter_fusion.5 = f32[3,2048]{0,1:T(8,128)S(1)} fusion(f32[3,2048]{0,1:T(8,128)S(1)} %scatter_fusion.4, s32[2048]{0:T(1024)S(1)} %bitcast.79, f32[2048,3]{1,0:T(8,128)S(1)} %copy.51), kind=kCustom, calls=%fused_computation.10 | custom fusion | flops 6144 | bytes 81920 | tf_op jit(solution)/shard_map/scatter-add | solution.py:145
  182.9 41.3 %psum.7 = f32[3,2048]{0,1:T(8,128)S(1)} all-reduce(f32[3,2048]{0,1:T(8,128)S(1)} %scatter_fusion.5), channel_id=1, replica_groups=mesh['rep'=4,'dom'=8] {'rep'}, use_global_device_ids=true, to_apply=%region_15.16 | all-reduce | flops 6144 | bytes 49152 | tf_op jit(solution)/shard_map/psum | solution.py:146
  (213 shorter events, 64.8 us)
Async XLA Ops:
  0.7 8.2 %copy-start.3 = (s32[1,1,128,1]{2,3,1,0:T(1,128)S(1)}, s32[1,1,128,1]{2,3,1,0:T(1,128)}, u32[]{:S(2)}) copy-start(s32[1,1,128,1]{2,3,1,0:T(1,128)} %param.17) | copy-start | bytes 1540
  0.7 8.4 %copy-start.4 = (s32[1,1,128]{2,1,0:T(1,128)S(1)}, s32[1,1,128]{2,1,0:T(1,128)}, u32[]{:S(2)}) copy-start(s32[1,1,128]{2,1,0:T(1,128)} %param.18) | copy-start | bytes 1540
  0.7 19.2 %copy-start.2 = (s32[3,2048]{1,0:T(4,128)S(1)}, s32[3,2048]{1,0:T(4,128)}, u32[]{:S(2)}) copy-start(s32[3,2048]{1,0:T(4,128)} %param.15) | copy-start | bytes 73732
  0.8 29.1 %copy-start.5 = (s32[1,1,128]{2,1,0:T(1,128)S(1)}, s32[1,1,128]{2,1,0:T(1,128)}, u32[]{:S(2)}) copy-start(s32[1,1,128]{2,1,0:T(1,128)} %param.16) | copy-start | bytes 1540
  0.8 34.2 %copy-start = (f32[3,2048]{1,0:T(4,128)S(1)}, f32[3,2048]{1,0:T(4,128)}, u32[]{:S(2)}) copy-start(f32[3,2048]{1,0:T(4,128)} %param.14) | copy-start | bytes 73732
  0.8 34.2 %copy-start.1 = (f32[3,2048]{1,0:T(4,128)S(1)}, f32[3,2048]{1,0:T(4,128)}, u32[]{:S(2)}) copy-start(f32[3,2048]{1,0:T(4,128)} %param.13) | copy-start | bytes 73732
  7.7 6.1 %collective-permute-start = (f32[16,3,128]{2,1,0:T(4,128)S(1)}, f32[16,3,128]{2,1,0:T(4,128)S(1)}, u32[]{:S(2)}, u32[]{:S(2)}) collective-permute-start(f32[16,3,128]{2,1,0:T(4,128)S(1)} %bitcast.78), channel_id=1, source_target_pairs={{0,1},{1,2},{2,3},{3,4},{4,5},{5,6},{6,7},{7,0},{8,9},{9,10},{10,1... | collective-permute-start | bytes 73736 | tf_op jit(solution)/shard_map/ppermute | solution.py:107
  13.9 5.5 %collective-permute-start.1 = (f32[16,3,128]{2,1,0:T(4,128)S(1)}, f32[16,3,128]{2,1,0:T(4,128)S(1)}, u32[]{:S(2)}, u32[]{:S(2)}) collective-permute-start(f32[16,3,128]{2,1,0:T(4,128)S(1)} %collective-permute-done), channel_id=1, source_target_pairs={{0,1},{1,2},{2,3},{3,4},{4,5},{5,6},{6,7},{7,0},{8,9},{9,10},{10,1... | collective-permute-start | bytes 73736 | tf_op jit(solution)/shard_map/ppermute | solution.py:107
  14.6 95.3 %all-to-all-start = ((f32[8,1,32]{2,1,0:T(1,128)}), f32[8,1,32]{2,1,0:T(1,128)S(1)}, u32[]{:S(2)}, u32[]{:S(2)}) async-start(f32[8,1,32]{2,1,0:T(1,128)} %convert_element_type.37), calls=%async_computation | async-start | bytes 8192 | tf_op jit(solution)/shard_map/all_to_all | solution.py:130
  19.4 5.3 %collective-permute-start.2 = (f32[16,3,128]{2,1,0:T(4,128)S(1)}, f32[16,3,128]{2,1,0:T(4,128)S(1)}, u32[]{:S(2)}, u32[]{:S(2)}) collective-permute-start(f32[16,3,128]{2,1,0:T(4,128)S(1)} %collective-permute-done.1), channel_id=1, source_target_pairs={{0,1},{1,2},{2,3},{3,4},{4,5},{5,6},{6,7},{7,0},{8,9},{9,10},{10,1... | collective-permute-start | bytes 73736 | tf_op jit(solution)/shard_map/ppermute | solution.py:107
  24.7 5.1 %collective-permute-start.3 = (f32[16,3,128]{2,1,0:T(4,128)S(1)}, f32[16,3,128]{2,1,0:T(4,128)S(1)}, u32[]{:S(2)}, u32[]{:S(2)}) collective-permute-start(f32[16,3,128]{2,1,0:T(4,128)S(1)} %collective-permute-done.2), channel_id=1, source_target_pairs={{0,1},{1,2},{2,3},{3,4},{4,5},{5,6},{6,7},{7,0},{8,9},{9,10},{10,1... | collective-permute-start | bytes 73736 | tf_op jit(solution)/shard_map/ppermute | solution.py:107
  29.8 5.1 %collective-permute-start.4 = (f32[16,3,128]{2,1,0:T(4,128)S(1)}, f32[16,3,128]{2,1,0:T(4,128)S(1)}, u32[]{:S(2)}, u32[]{:S(2)}) collective-permute-start(f32[16,3,128]{2,1,0:T(4,128)S(1)} %collective-permute-done.3), channel_id=1, source_target_pairs={{0,1},{1,2},{2,3},{3,4},{4,5},{5,6},{6,7},{7,0},{8,9},{9,10},{10,1... | collective-permute-start | bytes 73736 | tf_op jit(solution)/shard_map/ppermute | solution.py:107
  35.0 5.1 %collective-permute-start.5 = (f32[16,3,128]{2,1,0:T(4,128)S(1)}, f32[16,3,128]{2,1,0:T(4,128)S(1)}, u32[]{:S(2)}, u32[]{:S(2)}) collective-permute-start(f32[16,3,128]{2,1,0:T(4,128)S(1)} %collective-permute-done.4), channel_id=1, source_target_pairs={{0,1},{1,2},{2,3},{3,4},{4,5},{5,6},{6,7},{7,0},{8,9},{9,10},{10,1... | collective-permute-start | bytes 73736 | tf_op jit(solution)/shard_map/ppermute | solution.py:107
  40.1 5.1 %collective-permute-start.6 = (f32[16,3,128]{2,1,0:T(4,128)S(1)}, f32[16,3,128]{2,1,0:T(4,128)S(1)}, u32[]{:S(2)}, u32[]{:S(2)}) collective-permute-start(f32[16,3,128]{2,1,0:T(4,128)S(1)} %collective-permute-done.5), channel_id=1, source_target_pairs={{0,1},{1,2},{2,3},{3,4},{4,5},{5,6},{6,7},{7,0},{8,9},{9,10},{10,1... | collective-permute-start | bytes 73736 | tf_op jit(solution)/shard_map/ppermute | solution.py:107
  109.8 15.9 %all-to-all-start.1 = ((f32[8,32,3,128]{3,1,2,0:T(8,128)}), f32[8,32,3,128]{3,1,2,0:T(8,128)S(1)}, u32[]{:S(2)}, u32[]{:S(2)}) async-start(f32[8,32,3,128]{3,1,2,0:T(8,128)} %copy.47), calls=%async_computation.1 | async-start | bytes 786432 | tf_op jit(solution)/shard_map/all_to_all | solution.py:123
